TPU v7x, 256 devices: a whole 4x4x8 slice. The times are simulated.
256 devices in a mesh: nodes: 64 (over z, x, core), heads: 4 (over y).
Axes of the slice: x: 4, y: 4, z: 8, core: 2. Of those that a mesh axis runs over, the one named last changes fastest.
Arguments:
- nodes_in: bfloat16 [32768, 1024], P('nodes', 'heads'), may hold values from -6 to 6
- local_gain: float32 [1024], replicated, may hold values from 0.5 to 1.5
- neighbour_query_key_value: bfloat16 [3, 1024, 1024], P(None, None, 'heads'), may hold values from -0.25 to 0.25
- local_out: bfloat16 [1024, 1024], P('heads'), may hold values from -0.1875 to 0.1875
- global_gain: float32 [1024], replicated, may hold values from 0.5 to 1.5
- global_qkv: bfloat16 [3, 1024, 1024], P(None, None, 'heads'), may hold values from -0.1875 to 0.1875
- global_out: bfloat16 [1024, 1024], P('heads'), may hold values from -1.875 to 1.875
- feature_map: bfloat16 [16, 64, 128], P('heads'), may hold values from -5 to 5
- neighbour_count: int32 [256], P('nodes'), may hold values from 1 to 8
- neighbour_blocks: int32 [256, 8], P('nodes'), may hold values from 0 to 255, as said below
- metis_order: int32 [256], P('nodes'), may hold values from 0 to 255, as said below
- hashed_order: int32 [256], P('nodes'), may hold values from 0 to 255, as said below
Outputs:
- output: bfloat16 [32768, 1024], P('nodes', 'heads')
Inputs may be any that keep to these rules, and one draw needn't show every extreme that they name: `neighbour_blocks`: entry 0 of block b's list is b itself; every entry lies within 2 blocks of the aligned group of 4 blocks that holds b, inside the graph; entries from neighbour_count on are unused; entries may repeat. `metis_order`: A permutation of the block ids. `hashed_order`: A permutation of the block ids. The blocks at the 4 METIS positions of aligned group g go to the aligned groups of 4 hashed positions numbered (g + k * 16) modulo 64 for k = 0 to 3, exactly 1 of them to each; which block goes to which of these groups, and to which position in it, is drawn.
All inputs are finite; a program needn't handle non-finite values.
Results may differ from a plain program's by a relative error of at most 0.015.
Values may be sent and summed in bfloat16 or wider, within the bound.
No kernel may reach another device: no remote copies, remote signals or barrier semaphores. Data moves between devices by JAX's collectives and lax.ppermute only.
A program may use at most 64 MiB of HBM per device.

v0:
```python
import jax
import jax.numpy as jnp
from jax import lax
from jax.sharding import PartitionSpec as P

HD = 64
BLOCK = 128
HALO_BLK = 2
EPSILON = 1e-06


def passed_along(value, axis, steps):
    count = lax.axis_size(axis)
    pairs = [(source, (source + steps) % count) for source in range(count)]
    return lax.ppermute(value, axis, pairs)


def gathered_total(array, axis):
    parts = lax.all_gather(array, axis)
    return parts.sum(axis=0)


def laid_out(parts, dim):
    parts = jnp.moveaxis(parts, 0, dim)
    dims = parts.shape
    return parts.reshape(*dims[:dim], dims[dim] * dims[dim + 1], *dims[dim + 2 :])


def copy_for_each(array, axis):
    copies = jnp.broadcast_to(array, (lax.axis_size(axis), *array.shape))
    return lax.all_to_all(copies, axis, split_axis=0, concat_axis=0, tiled=True)


def collect(array, axis, dim):
    return laid_out(copy_for_each(array, axis), dim)


def padded(array, sides, width):
    for axis, dim in sides:
        count, length = (lax.axis_size(axis), array.shape[dim])
        up = [(i, (i + 1) % count) for i in range(count - 1)]
        down = [(j, i) for i, j in up]
        last = lax.slice_in_dim(array, length - width, length, axis=dim)
        initial = lax.slice_in_dim(array, 0, width, axis=dim)
        before = lax.ppermute(last, axis, up)
        after = lax.ppermute(initial, axis, down)
        array = jnp.concatenate([before, array, after], axis=dim)
    return array


def cut_along(array, dim, count):
    dims = array.shape
    parts = array.reshape(*dims[:dim], count, dims[dim] // count, *dims[dim + 1 :])
    return jnp.moveaxis(parts, dim, 0)


def summed_on_arrival(array, axis, dim):
    count = lax.axis_size(axis)
    parts = lax.all_to_all(cut_along(array, dim, count), axis, 0, 0, tiled=True)
    return jnp.sum(parts.astype(jnp.float32), axis=0)


def root_scale(row_data, gain_vector):
    as_float = row_data.astype(jnp.float32)
    mean_square = jnp.mean(as_float * as_float, axis=-1, keepdims=True)
    return (as_float * lax.rsqrt(mean_square + EPSILON) * gain_vector).astype(jnp.bfloat16)


def local_attention(queries, extended, counts, local_index):
    block_count = counts.shape[0]
    list_slots = local_index.shape[1]
    group_size = 4
    feature_width = queries.shape[1]
    heads_local = feature_width // HD
    key_blocks = extended.reshape(2, -1, BLOCK, feature_width)
    query_groups = queries.reshape(block_count // group_size, group_size, BLOCK, heads_local, HD)
    slot_of_key = jnp.arange(list_slots * BLOCK, dtype=jnp.int32) // BLOCK

    def one_group(inputs):
        query_group, index_group, count_group = inputs
        picked = key_blocks[:, index_group].reshape(
            2, group_size, list_slots * BLOCK, heads_local, HD
        )
        scores = jnp.einsum(
            "gqhd,gkhd->ghqk", query_group, picked[0], preferred_element_type=jnp.float32
        ) * HD ** (-0.5)
        live = slot_of_key[None, :] < count_group[:, None]
        scores = jnp.where(live[:, None, None, :], scores, -jnp.inf)
        row_max = jnp.max(scores, axis=-1, keepdims=True)
        expo = jnp.exp(scores - row_max)
        totals = jnp.sum(expo, axis=-1)
        local_weights = expo.astype(jnp.bfloat16)
        mixed_heads = jnp.einsum(
            "ghqk,gkhd->gqhd", local_weights, picked[1], preferred_element_type=jnp.float32
        )
        mixed_heads = mixed_heads / jnp.transpose(totals, (0, 2, 1))[..., None]
        return mixed_heads.astype(jnp.bfloat16)

    mixed_all = lax.map(
        one_group,
        (
            query_groups,
            local_index.reshape(block_count // group_size, group_size, list_slots),
            counts.reshape(block_count // group_size, group_size),
        ),
    )
    return mixed_all.reshape(block_count * BLOCK, feature_width)


def relayout(row_data, metis_local, all_hashed, device_nodes):
    block_count = metis_local.shape[0]
    devices = lax.axis_size("nodes")
    lane_count = min(block_count, devices)
    stride = max(1, devices // block_count)
    slot_limit = block_count // lane_count
    feature_width = row_data.shape[1]
    total_blocks = all_hashed.shape[0]
    matches = all_hashed[None, :] == metis_local[:, None]
    target = jnp.sum(
        jnp.where(matches, jnp.arange(total_blocks, dtype=jnp.int32)[None, :], 0), axis=1
    )
    steps_away = (target // block_count - device_nodes) % devices // stride
    order_ids = jnp.arange(block_count, dtype=jnp.int32)
    earlier = (steps_away[None, :] == steps_away[:, None]) & (
        order_ids[None, :] < order_ids[:, None]
    )
    rank_within = jnp.sum(earlier.astype(jnp.int32), axis=1)
    lane_id = rank_within * lane_count + steps_away
    chosen = lane_id[None, :] == order_ids[:, None]
    source = jnp.sum(jnp.where(chosen, order_ids[None, :], 0), axis=1)
    lane_target = jnp.sum(jnp.where(chosen, target[None, :], 0), axis=1)
    blocks = row_data.reshape(block_count, BLOCK, feature_width)
    outgoing = blocks[source].reshape(slot_limit, lane_count, BLOCK, feature_width)
    positions = lane_target.reshape(slot_limit, lane_count)
    block_pieces = [outgoing[:, :1]]
    position_pieces = [positions[:, :1]]
    for lane_step in range(1, lane_count):
        arrived, arrived_at = passed_along(
            (outgoing[:, lane_step : lane_step + 1], positions[:, lane_step : lane_step + 1]),
            "nodes",
            lane_step * stride,
        )
        block_pieces.append(arrived)
        position_pieces.append(arrived_at)
    incoming = jnp.concatenate(block_pieces, axis=1)
    in_position = jnp.concatenate(position_pieces, axis=1)
    local_position = in_position.reshape(block_count) - device_nodes * block_count
    located = local_position[None, :] == order_ids[:, None]
    picked_lane = jnp.sum(jnp.where(located, order_ids[None, :], 0), axis=1)
    return incoming.reshape(block_count, BLOCK, feature_width)[picked_lane].reshape(
        block_count * BLOCK, feature_width
    )


def gather_rows(shard_rows):
    return lax.all_gather(shard_rows, "heads", axis=1, tiled=True)


def global_mixing(full_rows, gain_vector, triple_weight, feature_map, out_weight):
    rescaled_input = root_scale(full_rows, gain_vector)
    triple = jnp.einsum(
        "au,nuz->naz", rescaled_input, triple_weight, preferred_element_type=jnp.float32
    ).astype(jnp.bfloat16)
    row_count = full_rows.shape[0]
    heads_local = feature_map.shape[0]

    def feature_maps(head_rows):
        angles = jnp.einsum(
            "nhd,hdf->nhf",
            head_rows.reshape(row_count, heads_local, HD),
            feature_map,
            preferred_element_type=jnp.float32,
        ) * HD ** (-0.5)
        return (jax.nn.elu(angles) + 1.0).astype(jnp.bfloat16)

    phi_query = feature_maps(triple[0])
    phi_key = feature_maps(triple[1])
    head_values = triple[2].reshape(row_count, heads_local, HD)
    summary = jnp.einsum("nhf,nhd->hfd", phi_key, head_values, preferred_element_type=jnp.float32)
    key_total = jnp.sum(phi_key.astype(jnp.float32), axis=0)
    summary, key_total = (gathered_total(summary, "nodes"), gathered_total(key_total, "nodes"))
    query_float = phi_query.astype(jnp.float32)
    numerator = jnp.einsum("nhf,hfd->nhd", query_float, summary, precision=lax.Precision.HIGHEST)
    denominator = jnp.einsum("nhf,hf->nh", query_float, key_total, precision=lax.Precision.HIGHEST)
    global_mixed = (
        (numerator / denominator[..., None])
        .astype(jnp.bfloat16)
        .reshape(row_count, heads_local * HD)
    )
    return jnp.dot(global_mixed, out_weight, preferred_element_type=jnp.float32)


def body(
    nodes_in,
    local_gain,
    neighbour_query_key_value,
    local_out,
    global_gain,
    global_qkv,
    global_out,
    feature_map,
    neighbour_count,
    neighbour_blocks,
    metis_order,
    hashed_order,
):
    block_count = metis_order.shape[0]
    device_nodes = lax.axis_index("nodes")
    all_hashed = collect(hashed_order, "nodes", 0)
    full_input = collect(nodes_in, "heads", 1)
    local_rescaled = root_scale(full_input, local_gain)
    triple = jnp.einsum(
        "au,nuz->naz", local_rescaled, neighbour_query_key_value, preferred_element_type=jnp.float32
    ).astype(jnp.bfloat16)
    rim_rows = HALO_BLK * BLOCK
    extended = padded(triple[1:], (("nodes", 1),), rim_rows)
    first_block = device_nodes * block_count - HALO_BLK
    local_index = neighbour_blocks - first_block
    local_mixed = local_attention(triple[0], extended, neighbour_count, local_index)
    partial_value = jnp.dot(local_mixed, local_out, preferred_element_type=jnp.float32)
    summed = lax.psum_scatter(
        partial_value.astype(jnp.bfloat16), "heads", scatter_dimension=1, tiled=True
    ).astype(jnp.float32)
    hidden = (nodes_in.astype(jnp.float32) + summed).astype(jnp.bfloat16)
    full_rows = gather_rows(hidden)
    global_partial = global_mixing(full_rows, global_gain, global_qkv, feature_map, global_out)
    global_summed = summed_on_arrival(global_partial.astype(jnp.bfloat16), "heads", 1)
    result = (hidden.astype(jnp.float32) + global_summed).astype(jnp.bfloat16)
    result = relayout(result, metis_order, all_hashed, device_nodes)
    return result


def solution(mesh):
    in_specs = (
        P("nodes", "heads"),
        P(),
        P(None, None, "heads"),
        P("heads", None),
        P(),
        P(None, None, "heads"),
        P("heads", None),
        P("heads", None, None),
        P("nodes"),
        P("nodes", None),
        P("nodes"),
        P("nodes"),
    )
    out_specs = P("nodes", "heads")
    return jax.shard_map(body, mesh=mesh, in_specs=in_specs, out_specs=out_specs, check_vma=False)
```

profile of v0, /device:TPU:33, one launch (start us, length us, event | category | flops | bytes accessed | tf_op | source)
XLA Modules:
  0.0 270.1 jit_solution(14255202605277190932)
XLA Ops:
  6.5 2.2 broadcast_in_dim.96
  8.7 4.2 %all-to-all-start = ((bf16[4,512,256]{2,1,0:T(8,128)(2,1)}), bf16[4,512,256]{2,1,0:T(8,128)(2,1)}, u32[]{:S(2)}, u32[]{:S(2)}) async-start(bf16[4,512,256]{2,1,0:T(8,128)(2,1)} %broadcast_in_dim.96), calls=%async_computation | async-start | bytes 2097152 | tf_op jit(solution)/shard_map/all_to_all | solution.py:31
  13.1 14.1 %all-to-all-done = bf16[4,512,256]{2,1,0:T(8,128)(2,1)} async-done(((bf16[4,512,256]{2,1,0:T(8,128)(2,1)}), bf16[4,512,256]{2,1,0:T(8,128)(2,1)}, u32[]{:S(2)}, u32[]{:S(2)}) %all-to-all-start) | async-done | bytes 1048608 | tf_op jit(solution)/shard_map/all_to_all | solution.py:31
  27.3 1.5 copy.35
  29.4 1.0 fusion.13
  30.5 3.7 %collective-permute-start.1 = (bf16[2,256,256]{2,1,0:T(8,128)(2,1)S(1)}, bf16[2,256,256]{2,1,0:T(8,128)(2,1)S(1)}, u32[]{:S(2)}, u32[]{:S(2)}) collective-permute-start(bf16[2,256,256]{2,1,0:T(8,128)(2,1)S(1)} %get-tuple-element.34), channel_id=1, source_target_pairs={{4,0},{8,4},{12,8},{16,12},{20,16},{24,20},{28,24},{32,28},{36,32}... | collective-permute-start | bytes 786440 | tf_op jit(solution)/shard_map/ppermute | solution.py:46
  34.2 3.0 %collective-permute-start = (bf16[2,256,256]{2,1,0:T(8,128)(2,1)S(1)}, bf16[2,256,256]{2,1,0:T(8,128)(2,1)}, u32[]{:S(2)}, u32[]{:S(2)}) collective-permute-start(bf16[2,256,256]{2,1,0:T(8,128)(2,1)S(1)} %get-tuple-element.33), channel_id=1, source_target_pairs={{0,4},{4,8},{8,12},{12,16},{16,20},{20,24},{24,28},{28,32},{32,36}... | collective-permute-start | bytes 786440 | tf_op jit(solution)/shard_map/ppermute | solution.py:45
  37.3 0.8 slice.81
  38.4 0.9 collective-permute-done.1
  39.3 1.2 collective-permute-done
  40.5 1.2 pad_maximum_fusion
  41.7 2.8 %gather_fusion = bf16[32,2,128,256]{3,2,1,0:T(8,128)(2,1)} fusion(bf16[2,8,128,256]{3,2,1,0:T(8,128)(2,1)S(1)} %bitcast.121, s32[1024]{0:T(1024)S(1)} %pad_clamp_fusion.2), kind=kCustom, calls=%fused_computation | custom fusion | bytes 8388736 | tf_op jit(solution)/shard_map/while/body/eval_jaxpr/gather | solution.py:81
  44.5 7.5 %copy.37 = bf16[4,8,2,128,256]{3,1,4,0,2:T(8,128)(2,1)} copy(bf16[4,8,2,128,256]{4,3,2,1,0:T(8,128)(2,1)} %bitcast.122) | data formatting | bytes 8388608 | tf_op jit(solution)/shard_map/while/body/eval_jaxpr/gather | solution.py:81
  52.0 4.5 %fusion.50 = (bf16[1,4,8,128,256]{3,2,4,1,0:T(8,128)(2,1)}, bf16[1,4,8,128,256]{3,2,4,1,0:T(8,128)(2,1)}) fusion(bf16[2,4,8,128,256]{3,2,4,1,0:T(8,128)(2,1)} %bitcast.123), kind=kLoop, calls=%fused_computation.104 | loop fusion | bytes 8388608 | tf_op jit(solution)/shard_map/while/body/eval_jaxpr/slice | solution.py:85
  56.5 4.2 %squeeze.19 = bf16[4,1024,4,64]{1,3,2,0:T(8,128)(2,1)} reshape(bf16[1,4,8,128,256]{3,2,4,1,0:T(8,128)(2,1)} %get-tuple-element.20) | data formatting | bytes 4194304 | tf_op jit(solution)/shard_map/while/body/eval_jaxpr/squeeze | solution.py:94
  60.7 4.2 %squeeze.21 = bf16[4,1024,4,64]{1,3,2,0:T(8,128)(2,1)} reshape(bf16[1,4,8,128,256]{3,2,4,1,0:T(8,128)(2,1)} %get-tuple-element.19) | data formatting | bytes 4194304 | tf_op jit(solution)/shard_map/while/body/eval_jaxpr/squeeze | solution.py:85
  64.8 2.9 %fusion = (f32[4,4,128]{2,1,0:T(4,128)S(1)}, f32[4,4,128,1024]{3,2,1,0:T(8,128)S(1)}) fusion(pred[4,1024]{1,0:T(4,128)(4,1)S(1)} %broadcast_compare_fusion, bf16[4,1024,4,64]{1,3,2,0:T(8,128)(2,1)} %squeeze.21, bf16[4,128,4,64]{3,2,1,0:T(4,128)(2,1)S(1)} %reshape.297), kind=kOutput, calls=%fused_computation.5 | convolution fusion | flops 274724864 | bytes 10760192 | tf_op jit(solution)/shard_map/while/body/eval_jaxpr/gqhd,gkhd->ghqk/dot_general | solution.py:84
  67.8 2.1 fusion.1
  69.9 2.2 fusion.34
  72.3 1.5 convolution_convert_fusion.1
  73.9 27.8 %reduce-scatter.2.cloned.1.call-done = bf16[512,256]{1,0:T(8,128)(2,1)} async-done(((bf16[512,1024]{1,0:T(8,128)(2,1)}), bf16[512,256]{1,0:T(8,128)(2,1)}) %reduce-scatter.2.cloned.1.call-update) | async-done | bytes 262160 | tf_op jit(solution)/shard_map/reduce_scatter | solution.py:221
  101.6 1.7 add_convert_fusion.1
  103.4 28.0 %all-gather.6.cloned.1.call-done = bf16[512,1024]{1,0:T(8,128)(2,1)} async-done(((bf16[512,256]{1,0:T(8,128)(2,1)}), bf16[512,1024]{1,0:T(8,128)(2,1)}) %all-gather.6.cloned.1.call-update) | async-done | bytes 1048592 | tf_op jit(solution)/shard_map/all_gather | solution.py:156
  131.4 1.5 fusion.6
  132.9 2.4 fusion.14
  135.4 0.8 convert_reduce_fusion.1
  136.2 0.9 fusion.56
  137.2 20.2 %all_to_all.16 = s32[64,1,4]{2,1,0:T(1,128)S(1)} all-to-all(s32[64,1,4]{2,1,0:T(1,128)S(1)} %broadcast_in_dim.100), channel_id=1, replica_groups=mesh['nodes'=64,'heads'=4] {'nodes'}, dimensions={0} | all-to-all | bytes 2048 | tf_op jit(solution)/shard_map/all_to_all | solution.py:31
  158.0 0.8 reduce.6
  159.4 48.5 %all-gather.2 = f32[64,4,128]{2,1,0:T(4,128)S(1)} all-gather(f32[1,4,128]{2,1,0:T(4,128)S(1)} %bitcast.138), channel_id=3, replica_groups=mesh['nodes'=64,'heads'=4] {'nodes'}, dimensions={0}, use_global_device_ids=true | all-gather | bytes 133120 | tf_op jit(solution)/shard_map/all_gather | solution.py:19
  208.0 0.7 fusion.27
  209.3 13.4 %all-gather.8.cloned.1.call-done = f32[256,128,64]{1,2,0:T(8,128)} async-done(((f32[4,128,64]{1,2,0:T(8,128)}), f32[256,128,64]{1,2,0:T(8,128)}) %all-gather.8.cloned.1.call-update) | async-done | bytes 8388624 | tf_op jit(solution)/shard_map/all_gather | solution.py:19
  222.7 3.9 %reduce_sum.116 = f32[4,128,64]{1,2,0:T(8,128)S(1)} reduce(f32[64,4,128,64]{2,3,1,0:T(8,128)} %bitcast.124, f32[]{:T(128)} %constant.91.clone.1), dimensions={0}, to_apply=%region_5.6 | reduce | flops 2064384 | bytes 8519684 | tf_op jit(solution)/shard_map/reduce_sum | solution.py:20
  226.6 0.7 fusion.19
  228.0 1.1 copy.62
  229.1 4.2 %all-to-all-start.1 = ((bf16[4,512,256]{2,1,0:T(8,128)(2,1)}), bf16[4,512,256]{2,1,0:T(8,128)(2,1)S(1)}, u32[]{:S(2)}, u32[]{:S(2)}) async-start(bf16[4,512,256]{2,1,0:T(8,128)(2,1)} %bitcast.126), calls=%async_computation.2 | async-start | bytes 2097152 | tf_op jit(solution)/shard_map/all_to_all | solution.py:59
  233.3 0.6 fusion.54
  233.9 1.8 collective-permute-start.7
  235.8 3.3 %collective-permute-start.6 = (s32[1,1]{1,0:T(1,128)}, s32[1,1]{1,0:T(1,128)}, u32[]{:S(2)}, u32[]{:S(2)}) collective-permute-start(s32[1,1]{1,0:T(1,128)} %get-tuple-element.41), channel_id=1, source_target_pairs={{0,128},{4,132},{8,136},{12,140},{16,144},{20,148},{24,152},{28,15... | collective-permute-start | bytes 20 | tf_op jit(solution)/shard_map/ppermute | solution.py:15
  239.1 3.2 %collective-permute-done.6 = s32[1,1]{1,0:T(1,128)} collective-permute-done((s32[1,1]{1,0:T(1,128)}, s32[1,1]{1,0:T(1,128)}, u32[]{:S(2)}, u32[]{:S(2)}) %collective-permute-start.6) | collective-permute-done | bytes 36 | tf_op jit(solution)/shard_map/ppermute | solution.py:15
  242.3 1.7 collective-permute-done.5
  243.9 2.6 add_subtract_fusion
  246.7 1.2 all-to-all-done.1
  248.7 1.9 collective-permute-start.4
  250.7 3.3 %collective-permute-start.3 = (bf16[1,1,128,256]{3,2,1,0:T(8,128)(2,1)S(1)}, bf16[1,1,128,256]{3,2,1,0:T(8,128)(2,1)S(1)}, u32[]{:S(2)}, u32[]{:S(2)}) collective-permute-start(bf16[1,1,128,256]{3,2,1,0:T(8,128)(2,1)S(1)} %get-tuple-element.37), channel_id=1, source_target_pairs={{0,128},{4,132},{8,136},{12,140},{16,144},{20,148},{24,152},{28,15... | collective-permute-start | bytes 196616 | tf_op jit(solution)/shard_map/ppermute | solution.py:15
  254.0 4.9 %collective-permute-done.3 = bf16[1,1,128,256]{3,2,1,0:T(8,128)(2,1)S(1)} collective-permute-done((bf16[1,1,128,256]{3,2,1,0:T(8,128)(2,1)S(1)}, bf16[1,1,128,256]{3,2,1,0:T(8,128)(2,1)S(1)}, u32[]{:S(2)}, u32[]{:S(2)}) %collective-permute-start.3) | collective-permute-done | bytes 65568 | tf_op jit(solution)/shard_map/ppermute | solution.py:15
  258.9 3.4 %collective-permute-done.2 = bf16[1,1,128,256]{3,2,1,0:T(8,128)(2,1)S(1)} collective-permute-done((bf16[1,1,128,256]{3,2,1,0:T(8,128)(2,1)S(1)}, bf16[1,1,128,256]{3,2,1,0:T(8,128)(2,1)S(1)}, u32[]{:S(2)}, u32[]{:S(2)}) %collective-permute-start.2) | collective-permute-done | bytes 65568 | tf_op jit(solution)/shard_map/ppermute | solution.py:15
  262.3 1.3 gather_fusion.2
  (74 shorter events, 5.2 us)
Async XLA Ops:
  6.5 22.8 %copy-start = (bf16[3,1024,256]{2,1,0:T(8,128)(2,1)S(1)}, bf16[3,1024,256]{2,1,0:T(8,128)(2,1)}, u32[]{:S(2)}) copy-start(bf16[3,1024,256]{2,1,0:T(8,128)(2,1)} %param.14) | copy-start | bytes 4718596
  6.5 6.5 %copy-start.7 = (s32[4,8]{1,0:T(4,128)S(1)}, s32[4,8]{1,0:T(4,128)}, u32[]{:S(2)}) copy-start(s32[4,8]{1,0:T(4,128)} %param.21) | copy-start | bytes 388
  8.7 18.6 %all-to-all-start = ((bf16[4,512,256]{2,1,0:T(8,128)(2,1)}), bf16[4,512,256]{2,1,0:T(8,128)(2,1)}, u32[]{:S(2)}, u32[]{:S(2)}) async-start(bf16[4,512,256]{2,1,0:T(8,128)(2,1)} %broadcast_in_dim.96), calls=%async_computation | async-start | bytes 2097152 | tf_op jit(solution)/shard_map/all_to_all | solution.py:31
  13.0 16.1 %copy-start.6 = (f32[1024]{0:T(1024)S(1)}, f32[1024]{0:T(1024)}, u32[]{:S(2)}) copy-start(f32[1024]{0:T(1024)} %param.13) | copy-start | bytes 12292
  13.0 88.7 %reduce-scatter.2.cloned.1.call-start = ((), (), s32[]{:S(2)}) async-start(), calls=%async_computation.4 | async-start | bytes 1310720 | tf_op jit(solution)/shard_map/reduce_scatter | solution.py:221
  29.4 7.9 %copy-start.9 = (s32[4]{0:T(128)S(1)}, s32[4]{0:T(128)}, u32[]{:S(2)}) copy-start(s32[4]{0:T(128)} %param.20) | copy-start | bytes 52
  30.5 8.9 %collective-permute-start.1 = (bf16[2,256,256]{2,1,0:T(8,128)(2,1)S(1)}, bf16[2,256,256]{2,1,0:T(8,128)(2,1)S(1)}, u32[]{:S(2)}, u32[]{:S(2)}) collective-permute-start(bf16[2,256,256]{2,1,0:T(8,128)(2,1)S(1)} %get-tuple-element.34), channel_id=1, source_target_pairs={{4,0},{8,4},{12,8},{16,12},{20,16},{24,20},{28,24},{32,28},{36,32}... | collective-permute-start | bytes 786440 | tf_op jit(solution)/shard_map/ppermute | solution.py:46
  34.2 6.3 %collective-permute-start = (bf16[2,256,256]{2,1,0:T(8,128)(2,1)S(1)}, bf16[2,256,256]{2,1,0:T(8,128)(2,1)}, u32[]{:S(2)}, u32[]{:S(2)}) collective-permute-start(bf16[2,256,256]{2,1,0:T(8,128)(2,1)S(1)} %get-tuple-element.33), channel_id=1, source_target_pairs={{0,4},{4,8},{8,12},{12,16},{16,20},{20,24},{24,28},{28,32},{32,36}... | collective-permute-start | bytes 786440 | tf_op jit(solution)/shard_map/ppermute | solution.py:45
  67.8 2.1 copy-start.2
  69.8 2.5 copy-start.4
  72.1 29.6 %copy-start.3 = (bf16[512,256]{1,0:T(8,128)(2,1)S(1)}, bf16[512,256]{1,0:T(8,128)(2,1)}, u32[]{:S(2)}) copy-start(bf16[512,256]{1,0:T(8,128)(2,1)} %param.12) | copy-start | bytes 786436
  72.3 60.6 %copy-start.11 = (bf16[3,1024,256]{2,1,0:T(8,128)(2,1)S(1)}, bf16[3,1024,256]{2,1,0:T(8,128)(2,1)}, u32[]{:S(2)}) copy-start(bf16[3,1024,256]{2,1,0:T(8,128)(2,1)} %param.17) | copy-start | bytes 4718596
  72.3 60.6 %copy-start.13 = (f32[1024]{0:T(1024)S(1)}, f32[1024]{0:T(1024)}, u32[]{:S(2)}) copy-start(f32[1024]{0:T(1024)} %param.16) | copy-start | bytes 12292
  73.8 57.6 %all-gather.6.cloned.1.call-start = ((), (), s32[]{:S(2)}) async-start(), calls=%async_computation.5 | async-start | bytes 1310720 | tf_op jit(solution)/shard_map/all_gather | solution.py:156
  103.4 119.3 %all-gather.8.cloned.1.call-start = ((), (), s32[]{:S(2)}) async-start(), calls=%async_computation.6 | async-start | bytes 8519680 | tf_op jit(solution)/shard_map/all_gather | solution.py:19
  132.9 2.5 copy-start.12
  135.4 1.7 copy-start.8
  135.4 23.4 %copy-start.10 = (s32[4]{0:T(128)S(1)}, s32[4]{0:T(128)}, u32[]{:S(2)}) copy-start(s32[4]{0:T(128)} %param.22) | copy-start | bytes 52
  226.5 1.0 copy-start.5
  229.1 19.0 %copy-start.1 = (bf16[512,256]{1,0:T(8,128)(2,1)S(1)}, bf16[512,256]{1,0:T(8,128)(2,1)}, u32[]{:S(2)}) copy-start(bf16[512,256]{1,0:T(8,128)(2,1)} %add_convert_fusion.1) | copy-start | bytes 786436
  229.1 18.8 %all-to-all-start.1 = ((bf16[4,512,256]{2,1,0:T(8,128)(2,1)}), bf16[4,512,256]{2,1,0:T(8,128)(2,1)S(1)}, u32[]{:S(2)}, u32[]{:S(2)}) async-start(bf16[4,512,256]{2,1,0:T(8,128)(2,1)} %bitcast.126), calls=%async_computation.2 | async-start | bytes 2097152 | tf_op jit(solution)/shard_map/all_to_all | solution.py:59
  233.9 5.2 %collective-permute-start.7 = (s32[1,1]{1,0:T(1,128)}, s32[1,1]{1,0:T(1,128)}, u32[]{:S(2)}, u32[]{:S(2)}) collective-permute-start(s32[1,1]{1,0:T(1,128)} %get-tuple-element.40), channel_id=1, source_target_pairs={{0,192},{4,196},{8,200},{12,204},{16,208},{20,212},{24,216},{28,22... | collective-permute-start | bytes 20 | tf_op jit(solution)/shard_map/ppermute | solution.py:15
  235.8 6.5 %collective-permute-start.6 = (s32[1,1]{1,0:T(1,128)}, s32[1,1]{1,0:T(1,128)}, u32[]{:S(2)}, u32[]{:S(2)}) collective-permute-start(s32[1,1]{1,0:T(1,128)} %get-tuple-element.41), channel_id=1, source_target_pairs={{0,128},{4,132},{8,136},{12,140},{16,144},{20,148},{24,152},{28,15... | collective-permute-start | bytes 20 | tf_op jit(solution)/shard_map/ppermute | solution.py:15
  239.1 4.8 %collective-permute-start.5 = (s32[1,1]{1,0:T(1,128)}, s32[1,1]{1,0:T(1,128)}, u32[]{:S(2)}, u32[]{:S(2)}) collective-permute-start(s32[1,1]{1,0:T(1,128)} %get-tuple-element.42), channel_id=1, source_target_pairs={{0,64},{4,68},{8,72},{12,76},{16,80},{20,84},{24,88},{28,92},{32,9... | collective-permute-start | bytes 20 | tf_op jit(solution)/shard_map/ppermute | solution.py:15
  248.7 5.2 %collective-permute-start.4 = (bf16[1,1,128,256]{3,2,1,0:T(8,128)(2,1)S(1)}, bf16[1,1,128,256]{3,2,1,0:T(8,128)(2,1)S(1)}, u32[]{:S(2)}, u32[]{:S(2)}) collective-permute-start(bf16[1,1,128,256]{3,2,1,0:T(8,128)(2,1)S(1)} %get-tuple-element.36), channel_id=1, source_target_pairs={{0,192},{4,196},{8,200},{12,204},{16,208},{20,212},{24,216},{28,22... | collective-permute-start | bytes 196616 | tf_op jit(solution)/shard_map/ppermute | solution.py:15
  250.7 8.2 %collective-permute-start.3 = (bf16[1,1,128,256]{3,2,1,0:T(8,128)(2,1)S(1)}, bf16[1,1,128,256]{3,2,1,0:T(8,128)(2,1)S(1)}, u32[]{:S(2)}, u32[]{:S(2)}) collective-permute-start(bf16[1,1,128,256]{3,2,1,0:T(8,128)(2,1)S(1)} %get-tuple-element.37), channel_id=1, source_target_pairs={{0,128},{4,132},{8,136},{12,140},{16,144},{20,148},{24,152},{28,15... | collective-permute-start | bytes 196616 | tf_op jit(solution)/shard_map/ppermute | solution.py:15
  254.0 8.3 %collective-permute-start.2 = (bf16[1,1,128,256]{3,2,1,0:T(8,128)(2,1)S(1)}, bf16[1,1,128,256]{3,2,1,0:T(8,128)(2,1)S(1)}, u32[]{:S(2)}, u32[]{:S(2)}) collective-permute-start(bf16[1,1,128,256]{3,2,1,0:T(8,128)(2,1)S(1)} %get-tuple-element.38), channel_id=1, source_target_pairs={{0,64},{4,68},{8,72},{12,76},{16,80},{20,84},{24,88},{28,92},{32,9... | collective-permute-start | bytes 196616 | tf_op jit(solution)/shard_map/ppermute | solution.py:15
Sparse Core Ops, SparseCore 0:
  73.9 27.6 reduce-scatter.1
  103.5 27.8 all-gather.5
  137.2 85.3 all-gather.7
where the time goes:
time: 271 us; the launch traced here: 270 us
  waiting for transfers between devices  99.8 us (37%)
  blocking collectives  68.7 us (25%)
  local copies, waits for them, and re-layouts  33 us (12%)
  starting transfers between devices  25.6 us (9%)
  other arithmetic  15.4 us (6%)
  matrix products  14 us (5%)
  between operations  13.5 us (5%)
    all_gather x1, blocking collectives, gathered_total(): parts = lax.all_gather(array, axis)  48.5 us
    all_gather x1, waiting for transfers between devices, gather_rows(): return lax.all_gather(shard_rows, 'heads', axis=1, tiled=True)  28 us
    reduce_scatter x1, waiting for transfers between devices, body(): lax.psum_scatter(partial_value.astype(jnp.bfloat16), 'heads', scatter_dim...  27.8 us
    all_to_all x1, blocking collectives, copy_for_each(): return lax.all_to_all(copies, axis, split_axis=0, concat_axis=0, tiled=True)  20.2 us
    all_to_all x1, waiting for transfers between devices, copy_for_each(): return lax.all_to_all(copies, axis, split_axis=0, concat_axis=0, tiled=True)  14.1 us
    all_gather x1, waiting for transfers between devices, gathered_total(): parts = lax.all_gather(array, axis)  13.4 us
    ppermute x6, waiting for transfers between devices, passed_along(): return lax.ppermute(value, axis, pairs)  13.1 us
    ppermute x6, starting transfers between devices, passed_along(): return lax.ppermute(value, axis, pairs)  10.4 us
  transfers between devices with their start and end apart: 13, of which 11 were waited for; matrix products, arithmetic and copies ran while one was open for 3% of the time, Pallas kernels for 0%

commit v1 on v0

--- a/solution.py
+++ b/solution.py
@@ -153,7 +153,9 @@
 
 
 def gather_rows(shard_rows):
-    return lax.all_gather(shard_rows, "heads", axis=1, tiled=True)
+    return jnp.concatenate(
+        lax.all_to_all(jnp.stack([shard_rows] * lax.axis_size("heads")), "heads", 0, 0), axis=1
+    )
 
 
 def global_mixing(full_rows, gain_vector, triple_weight, feature_map, out_weight):

time: 271 us -> 258 us (0.952)
  waiting for transfers between devices: 99.8 us -> 70.6 us
  blocking collectives: 68.7 us -> 86 us
    all_gather x1 -> x0, waiting for transfers between devices: 28 us -> none  [gather_rows(): return lax.all_gather(shard_rows, 'heads', axis=1, tiled=True)]
    all_to_all x0 -> x1, blocking collectives: none -> 15.8 us  [gather_rows(): lax.all_to_all(jnp.stack([shard_rows] * lax.axis_size('heads')), 'heads',...]
  transfers between devices with their start and end apart: 13 -> 12, of which waited for: 11 -> 10; matrix products, arithmetic and copies ran while one was open for 3% -> 3% of each run, Pallas kernels for 0% -> 0%
where the time goes in v1:
time: 258 us; the launch traced here: 257 us
  blocking collectives  86 us (33%)
  waiting for transfers between devices  70.6 us (27%)
  local copies, waits for them, and re-layouts  35.3 us (14%)
  starting transfers between devices  25.5 us (10%)
  between operations  13.8 us (5%)
  other arithmetic  13.7 us (5%)
  matrix products  12.7 us (5%)
    all_gather x1, blocking collectives, gathered_total(): parts = lax.all_gather(array, axis)  48.5 us
    reduce_scatter x1, waiting for transfers between devices, body(): lax.psum_scatter(partial_value.astype(jnp.bfloat16), 'heads', scatter_dim...  27.8 us
    all_to_all x1, blocking collectives, copy_for_each(): return lax.all_to_all(copies, axis, split_axis=0, concat_axis=0, tiled=True)  21.7 us
    all_to_all x1, blocking collectives, gather_rows(): lax.all_to_all(jnp.stack([shard_rows] * lax.axis_size('heads')), 'heads',...  15.8 us
    all_to_all x1, waiting for transfers between devices, copy_for_each(): return lax.all_to_all(copies, axis, split_axis=0, concat_axis=0, tiled=True)  14.1 us
    ppermute x6, waiting for transfers between devices, passed_along(): return lax.ppermute(value, axis, pairs)  13.1 us
    all_gather x1, waiting for transfers between devices, gathered_total(): parts = lax.all_gather(array, axis)  12 us
    ppermute x6, starting transfers between devices, passed_along(): return lax.ppermute(value, axis, pairs)  10.4 us
  transfers between devices with their start and end apart: 12, of which 10 were waited for; matrix products, arithmetic and copies ran while one was open for 3% of the time, Pallas kernels for 0%

profile of v1, /device:TPU:33, one launch (start us, length us, event | category | flops | bytes accessed | tf_op | source)
XLA Modules:
  0.0 257.4 jit_solution(4572680112606435435)
XLA Ops:
  6.5 2.2 broadcast_in_dim.96
  8.7 4.2 %all-to-all-start = ((bf16[4,512,256]{2,1,0:T(8,128)(2,1)}), bf16[4,512,256]{2,1,0:T(8,128)(2,1)}, u32[]{:S(2)}, u32[]{:S(2)}) async-start(bf16[4,512,256]{2,1,0:T(8,128)(2,1)} %broadcast_in_dim.96), calls=%async_computation | async-start | bytes 2097152 | tf_op jit(solution)/shard_map/all_to_all | solution.py:31
  13.1 14.1 %all-to-all-done = bf16[4,512,256]{2,1,0:T(8,128)(2,1)} async-done(((bf16[4,512,256]{2,1,0:T(8,128)(2,1)}), bf16[4,512,256]{2,1,0:T(8,128)(2,1)}, u32[]{:S(2)}, u32[]{:S(2)}) %all-to-all-start) | async-done | bytes 1048608 | tf_op jit(solution)/shard_map/all_to_all | solution.py:31
  27.3 1.5 copy.37
  29.4 1.0 fusion.12
  30.5 3.7 %collective-permute-start.1 = (bf16[2,256,256]{2,1,0:T(8,128)(2,1)S(1)}, bf16[2,256,256]{2,1,0:T(8,128)(2,1)S(1)}, u32[]{:S(2)}, u32[]{:S(2)}) collective-permute-start(bf16[2,256,256]{2,1,0:T(8,128)(2,1)S(1)} %get-tuple-element.34), channel_id=1, source_target_pairs={{4,0},{8,4},{12,8},{16,12},{20,16},{24,20},{28,24},{32,28},{36,32}... | collective-permute-start | bytes 786440 | tf_op jit(solution)/shard_map/ppermute | solution.py:46
  34.2 3.0 %collective-permute-start = (bf16[2,256,256]{2,1,0:T(8,128)(2,1)S(1)}, bf16[2,256,256]{2,1,0:T(8,128)(2,1)}, u32[]{:S(2)}, u32[]{:S(2)}) collective-permute-start(bf16[2,256,256]{2,1,0:T(8,128)(2,1)S(1)} %get-tuple-element.33), channel_id=1, source_target_pairs={{0,4},{4,8},{8,12},{12,16},{16,20},{20,24},{24,28},{28,32},{32,36}... | collective-permute-start | bytes 786440 | tf_op jit(solution)/shard_map/ppermute | solution.py:45
  37.3 0.8 slice.81
  38.4 0.9 collective-permute-done.1
  39.3 1.2 collective-permute-done
  40.5 1.2 pad_maximum_fusion
  41.7 2.8 %gather_fusion = bf16[32,2,128,256]{3,2,1,0:T(8,128)(2,1)} fusion(bf16[2,8,128,256]{3,2,1,0:T(8,128)(2,1)S(1)} %bitcast.129, s32[1024]{0:T(1024)S(1)} %pad_clamp_fusion.2), kind=kCustom, calls=%fused_computation | custom fusion | bytes 8388736 | tf_op jit(solution)/shard_map/while/body/eval_jaxpr/gather | solution.py:81
  44.5 7.5 %copy.39 = bf16[4,8,2,128,256]{3,1,4,0,2:T(8,128)(2,1)} copy(bf16[4,8,2,128,256]{4,3,2,1,0:T(8,128)(2,1)} %bitcast.130) | data formatting | bytes 8388608 | tf_op jit(solution)/shard_map/while/body/eval_jaxpr/gather | solution.py:81
  52.0 4.5 %fusion.46 = (bf16[1,4,8,128,256]{3,2,4,1,0:T(8,128)(2,1)}, bf16[1,4,8,128,256]{3,2,4,1,0:T(8,128)(2,1)}) fusion(bf16[2,4,8,128,256]{3,2,4,1,0:T(8,128)(2,1)} %bitcast.131), kind=kLoop, calls=%fused_computation.101 | loop fusion | bytes 8388608 | tf_op jit(solution)/shard_map/while/body/eval_jaxpr/slice | solution.py:85
  56.5 4.2 %squeeze.19 = bf16[4,1024,4,64]{1,3,2,0:T(8,128)(2,1)} reshape(bf16[1,4,8,128,256]{3,2,4,1,0:T(8,128)(2,1)} %get-tuple-element.20) | data formatting | bytes 4194304 | tf_op jit(solution)/shard_map/while/body/eval_jaxpr/squeeze | solution.py:94
  60.7 4.2 %squeeze.21 = bf16[4,1024,4,64]{1,3,2,0:T(8,128)(2,1)} reshape(bf16[1,4,8,128,256]{3,2,4,1,0:T(8,128)(2,1)} %get-tuple-element.19) | data formatting | bytes 4194304 | tf_op jit(solution)/shard_map/while/body/eval_jaxpr/squeeze | solution.py:85
  64.8 2.9 %fusion = (f32[4,4,128]{2,1,0:T(4,128)S(1)}, f32[4,4,128,1024]{3,2,1,0:T(8,128)S(1)}) fusion(pred[4,1024]{1,0:T(4,128)(4,1)S(1)} %broadcast_compare_fusion, bf16[4,1024,4,64]{1,3,2,0:T(8,128)(2,1)} %squeeze.21, bf16[4,128,4,64]{3,2,1,0:T(4,128)(2,1)S(1)} %reshape.304), kind=kOutput, calls=%fused_computation.5 | convolution fusion | flops 274724864 | bytes 10760192 | tf_op jit(solution)/shard_map/while/body/eval_jaxpr/gqhd,gkhd->ghqk/dot_general | solution.py:84
  67.8 2.1 fusion.1
  69.9 2.2 fusion.30
  72.3 1.5 convolution_convert_fusion.1
  73.9 27.8 %reduce-scatter.2.cloned.1.call-done = bf16[512,256]{1,0:T(8,128)(2,1)} async-done(((bf16[512,1024]{1,0:T(8,128)(2,1)}), bf16[512,256]{1,0:T(8,128)(2,1)}) %reduce-scatter.2.cloned.1.call-update) | async-done | bytes 262160 | tf_op jit(solution)/shard_map/reduce_scatter | solution.py:223
  101.6 1.0 add_convert_fusion.1
  102.7 15.8 %all_to_all.21 = bf16[4,512,256]{2,1,0:T(8,128)(2,1)} all-to-all(bf16[4,512,256]{2,1,0:T(8,128)(2,1)S(1)} %stack.2), channel_id=1, replica_groups=mesh['nodes'=64,'heads'=4] {'heads'}, dimensions={0} | all-to-all | bytes 2097152 | tf_op jit(solution)/shard_map/all_to_all | solution.py:157
  118.6 1.5 copy.43
  120.7 0.8 copy-done.11
  121.5 1.0 fusion.13
  122.6 0.8 convert_reduce_fusion.1
  123.4 0.9 fusion.52
  124.3 21.7 %all_to_all.22 = s32[64,1,4]{2,1,0:T(1,128)S(1)} all-to-all(s32[64,1,4]{2,1,0:T(1,128)S(1)} %broadcast_in_dim.100), channel_id=1, replica_groups=mesh['nodes'=64,'heads'=4] {'nodes'}, dimensions={0} | all-to-all | bytes 2048 | tf_op jit(solution)/shard_map/all_to_all | solution.py:31
  147.8 48.5 %all-gather.2 = f32[64,4,128]{2,1,0:T(4,128)S(1)} all-gather(f32[1,4,128]{2,1,0:T(4,128)S(1)} %bitcast.146), channel_id=3, replica_groups=mesh['nodes'=64,'heads'=4] {'nodes'}, dimensions={0}, use_global_device_ids=true | all-gather | bytes 133120 | tf_op jit(solution)/shard_map/all_gather | solution.py:19
  196.4 0.7 fusion.24
  197.6 12.0 %all-gather.5.cloned.1.call-done = f32[256,128,64]{1,2,0:T(8,128)} async-done(((f32[4,128,64]{1,2,0:T(8,128)}), f32[256,128,64]{1,2,0:T(8,128)}) %all-gather.5.cloned.1.call-update) | async-done | bytes 8388624 | tf_op jit(solution)/shard_map/all_gather | solution.py:19
  209.7 3.9 %reduce_sum.116 = f32[4,128,64]{1,2,0:T(8,128)S(1)} reduce(f32[64,4,128,64]{2,3,1,0:T(8,128)} %bitcast.132, f32[]{:T(128)} %constant.91.clone.1), dimensions={0}, to_apply=%region_5.6 | reduce | flops 2064384 | bytes 8519684 | tf_op jit(solution)/shard_map/reduce_sum | solution.py:20
  213.5 0.7 fusion.18
  215.0 1.1 copy.68
  216.1 4.0 %all-to-all-start.2 = ((bf16[4,512,256]{2,1,0:T(8,128)(2,1)}), bf16[4,512,256]{2,1,0:T(8,128)(2,1)S(1)}, u32[]{:S(2)}, u32[]{:S(2)}) async-start(bf16[4,512,256]{2,1,0:T(8,128)(2,1)} %bitcast.134), calls=%async_computation.3 | async-start | bytes 2097152 | tf_op jit(solution)/shard_map/all_to_all | solution.py:59
  220.1 0.7 fusion.50
  220.8 1.8 collective-permute-start.7
  222.6 3.3 %collective-permute-start.6 = (s32[1,1]{1,0:T(1,128)}, s32[1,1]{1,0:T(1,128)}, u32[]{:S(2)}, u32[]{:S(2)}) collective-permute-start(s32[1,1]{1,0:T(1,128)} %get-tuple-element.41), channel_id=1, source_target_pairs={{0,128},{4,132},{8,136},{12,140},{16,144},{20,148},{24,152},{28,15... | collective-permute-start | bytes 20 | tf_op jit(solution)/shard_map/ppermute | solution.py:15
  226.0 3.0 %collective-permute-done.6 = s32[1,1]{1,0:T(1,128)} collective-permute-done((s32[1,1]{1,0:T(1,128)}, s32[1,1]{1,0:T(1,128)}, u32[]{:S(2)}, u32[]{:S(2)}) %collective-permute-start.6) | collective-permute-done | bytes 36 | tf_op jit(solution)/shard_map/ppermute | solution.py:15
  229.0 1.7 collective-permute-done.5
  230.6 2.6 %add_subtract_fusion = s32[4]{0:T(128)S(1)} fusion(s32[1]{0:T(128)} %bitcast.36, s32[1]{0:T(128)} %bitcast.35, s32[1]{0:T(128)} %bitcast.34, s32[1]{0:T(128)} %bitcast.33, s32[]{:T(128)S(6)} %mul.74), kind=kLoop, calls=%fused_computation.97 | loop fusion | flops 16 | bytes 36 | tf_op jit(solution)/shard_map/sub | solution.py:147
  233.4 1.4 all-to-all-done.2
  235.6 1.9 collective-permute-start.4
  237.5 3.3 %collective-permute-start.3 = (bf16[1,1,128,256]{3,2,1,0:T(8,128)(2,1)S(1)}, bf16[1,1,128,256]{3,2,1,0:T(8,128)(2,1)S(1)}, u32[]{:S(2)}, u32[]{:S(2)}) collective-permute-start(bf16[1,1,128,256]{3,2,1,0:T(8,128)(2,1)S(1)} %get-tuple-element.37), channel_id=1, source_target_pairs={{0,128},{4,132},{8,136},{12,140},{16,144},{20,148},{24,152},{28,15... | collective-permute-start | bytes 196616 | tf_op jit(solution)/shard_map/ppermute | solution.py:15
  240.8 4.8 %collective-permute-done.3 = bf16[1,1,128,256]{3,2,1,0:T(8,128)(2,1)S(1)} collective-permute-done((bf16[1,1,128,256]{3,2,1,0:T(8,128)(2,1)S(1)}, bf16[1,1,128,256]{3,2,1,0:T(8,128)(2,1)S(1)}, u32[]{:S(2)}, u32[]{:S(2)}) %collective-permute-start.3) | collective-permute-done | bytes 65568 | tf_op jit(solution)/shard_map/ppermute | solution.py:15
  245.6 3.7 %collective-permute-done.2 = bf16[1,1,128,256]{3,2,1,0:T(8,128)(2,1)S(1)} collective-permute-done((bf16[1,1,128,256]{3,2,1,0:T(8,128)(2,1)S(1)}, bf16[1,1,128,256]{3,2,1,0:T(8,128)(2,1)S(1)}, u32[]{:S(2)}, u32[]{:S(2)}) %collective-permute-start.2) | collective-permute-done | bytes 65568 | tf_op jit(solution)/shard_map/ppermute | solution.py:15
  249.3 1.3 gather_fusion.2
  (73 shorter events, 6.4 us)
Async XLA Ops:
  6.5 22.8 %copy-start = (bf16[3,1024,256]{2,1,0:T(8,128)(2,1)S(1)}, bf16[3,1024,256]{2,1,0:T(8,128)(2,1)}, u32[]{:S(2)}) copy-start(bf16[3,1024,256]{2,1,0:T(8,128)(2,1)} %param.14) | copy-start | bytes 4718596
  6.5 6.5 %copy-start.7 = (s32[4,8]{1,0:T(4,128)S(1)}, s32[4,8]{1,0:T(4,128)}, u32[]{:S(2)}) copy-start(s32[4,8]{1,0:T(4,128)} %param.21) | copy-start | bytes 388
  8.7 18.6 %all-to-all-start = ((bf16[4,512,256]{2,1,0:T(8,128)(2,1)}), bf16[4,512,256]{2,1,0:T(8,128)(2,1)}, u32[]{:S(2)}, u32[]{:S(2)}) async-start(bf16[4,512,256]{2,1,0:T(8,128)(2,1)} %broadcast_in_dim.96), calls=%async_computation | async-start | bytes 2097152 | tf_op jit(solution)/shard_map/all_to_all | solution.py:31
  13.0 16.1 %copy-start.5 = (f32[1024]{0:T(1024)S(1)}, f32[1024]{0:T(1024)}, u32[]{:S(2)}) copy-start(f32[1024]{0:T(1024)} %param.13) | copy-start | bytes 12292
  13.0 88.6 %reduce-scatter.2.cloned.1.call-start = ((), (), s32[]{:S(2)}) async-start(), calls=%async_computation.5 | async-start | bytes 1310720 | tf_op jit(solution)/shard_map/reduce_scatter | solution.py:223
  29.4 7.9 %copy-start.9 = (s32[4]{0:T(128)S(1)}, s32[4]{0:T(128)}, u32[]{:S(2)}) copy-start(s32[4]{0:T(128)} %param.20) | copy-start | bytes 52
  30.5 8.9 %collective-permute-start.1 = (bf16[2,256,256]{2,1,0:T(8,128)(2,1)S(1)}, bf16[2,256,256]{2,1,0:T(8,128)(2,1)S(1)}, u32[]{:S(2)}, u32[]{:S(2)}) collective-permute-start(bf16[2,256,256]{2,1,0:T(8,128)(2,1)S(1)} %get-tuple-element.34), channel_id=1, source_target_pairs={{4,0},{8,4},{12,8},{16,12},{20,16},{24,20},{28,24},{32,28},{36,32}... | collective-permute-start | bytes 786440 | tf_op jit(solution)/shard_map/ppermute | solution.py:46
  34.2 6.3 %collective-permute-start = (bf16[2,256,256]{2,1,0:T(8,128)(2,1)S(1)}, bf16[2,256,256]{2,1,0:T(8,128)(2,1)}, u32[]{:S(2)}, u32[]{:S(2)}) collective-permute-start(bf16[2,256,256]{2,1,0:T(8,128)(2,1)S(1)} %get-tuple-element.33), channel_id=1, source_target_pairs={{0,4},{4,8},{8,12},{12,16},{16,20},{20,24},{24,28},{28,32},{32,36}... | collective-permute-start | bytes 786440 | tf_op jit(solution)/shard_map/ppermute | solution.py:45
  67.8 2.1 copy-start.1
  69.8 2.5 copy-start.3
  72.1 29.5 %copy-start.2 = (bf16[512,256]{1,0:T(8,128)(2,1)S(1)}, bf16[512,256]{1,0:T(8,128)(2,1)}, u32[]{:S(2)}) copy-start(bf16[512,256]{1,0:T(8,128)(2,1)} %param.12) | copy-start | bytes 786436
  73.8 135.9 %all-gather.5.cloned.1.call-start = ((), (), s32[]{:S(2)}) async-start(), calls=%async_computation.6 | async-start | bytes 8519680 | tf_op jit(solution)/shard_map/all_gather | solution.py:19
  118.6 1.8 copy-start.6
  120.1 1.4 copy-start.11
  121.5 1.1 copy-start.12
  122.6 1.7 copy-start.8
  122.6 24.7 %copy-start.10 = (s32[4]{0:T(128)S(1)}, s32[4]{0:T(128)}, u32[]{:S(2)}) copy-start(s32[4]{0:T(128)} %param.22) | copy-start | bytes 52
  213.5 1.0 copy-start.4
  216.1 18.7 %all-to-all-start.2 = ((bf16[4,512,256]{2,1,0:T(8,128)(2,1)}), bf16[4,512,256]{2,1,0:T(8,128)(2,1)S(1)}, u32[]{:S(2)}, u32[]{:S(2)}) async-start(bf16[4,512,256]{2,1,0:T(8,128)(2,1)} %bitcast.134), calls=%async_computation.3 | async-start | bytes 2097152 | tf_op jit(solution)/shard_map/all_to_all | solution.py:59
  220.8 5.2 %collective-permute-start.7 = (s32[1,1]{1,0:T(1,128)}, s32[1,1]{1,0:T(1,128)}, u32[]{:S(2)}, u32[]{:S(2)}) collective-permute-start(s32[1,1]{1,0:T(1,128)} %get-tuple-element.40), channel_id=1, source_target_pairs={{0,192},{4,196},{8,200},{12,204},{16,208},{20,212},{24,216},{28,22... | collective-permute-start | bytes 20 | tf_op jit(solution)/shard_map/ppermute | solution.py:15
  222.6 6.3 %collective-permute-start.6 = (s32[1,1]{1,0:T(1,128)}, s32[1,1]{1,0:T(1,128)}, u32[]{:S(2)}, u32[]{:S(2)}) collective-permute-start(s32[1,1]{1,0:T(1,128)} %get-tuple-element.41), channel_id=1, source_target_pairs={{0,128},{4,132},{8,136},{12,140},{16,144},{20,148},{24,152},{28,15... | collective-permute-start | bytes 20 | tf_op jit(solution)/shard_map/ppermute | solution.py:15
  226.0 4.7 %collective-permute-start.5 = (s32[1,1]{1,0:T(1,128)}, s32[1,1]{1,0:T(1,128)}, u32[]{:S(2)}, u32[]{:S(2)}) collective-permute-start(s32[1,1]{1,0:T(1,128)} %get-tuple-element.42), channel_id=1, source_target_pairs={{0,64},{4,68},{8,72},{12,76},{16,80},{20,84},{24,88},{28,92},{32,9... | collective-permute-start | bytes 20 | tf_op jit(solution)/shard_map/ppermute | solution.py:15
  235.6 5.2 %collective-permute-start.4 = (bf16[1,1,128,256]{3,2,1,0:T(8,128)(2,1)S(1)}, bf16[1,1,128,256]{3,2,1,0:T(8,128)(2,1)S(1)}, u32[]{:S(2)}, u32[]{:S(2)}) collective-permute-start(bf16[1,1,128,256]{3,2,1,0:T(8,128)(2,1)S(1)} %get-tuple-element.36), channel_id=1, source_target_pairs={{0,192},{4,196},{8,200},{12,204},{16,208},{20,212},{24,216},{28,22... | collective-permute-start | bytes 196616 | tf_op jit(solution)/shard_map/ppermute | solution.py:15
  237.5 8.1 %collective-permute-start.3 = (bf16[1,1,128,256]{3,2,1,0:T(8,128)(2,1)S(1)}, bf16[1,1,128,256]{3,2,1,0:T(8,128)(2,1)S(1)}, u32[]{:S(2)}, u32[]{:S(2)}) collective-permute-start(bf16[1,1,128,256]{3,2,1,0:T(8,128)(2,1)S(1)} %get-tuple-element.37), channel_id=1, source_target_pairs={{0,128},{4,132},{8,136},{12,140},{16,144},{20,148},{24,152},{28,15... | collective-permute-start | bytes 196616 | tf_op jit(solution)/shard_map/ppermute | solution.py:15
  240.8 8.5 %collective-permute-start.2 = (bf16[1,1,128,256]{3,2,1,0:T(8,128)(2,1)S(1)}, bf16[1,1,128,256]{3,2,1,0:T(8,128)(2,1)S(1)}, u32[]{:S(2)}, u32[]{:S(2)}) collective-permute-start(bf16[1,1,128,256]{3,2,1,0:T(8,128)(2,1)S(1)} %get-tuple-element.38), channel_id=1, source_target_pairs={{0,64},{4,68},{8,72},{12,76},{16,80},{20,84},{24,88},{28,92},{32,9... | collective-permute-start | bytes 196616 | tf_op jit(solution)/shard_map/ppermute | solution.py:15
Sparse Core Ops, SparseCore 0:
  73.9 27.6 reduce-scatter.1
  124.4 85.2 all-gather.4
